TPU v7x, 32 devices: a whole 2x2x4 slice. The times are simulated.
32 devices in a mesh: group: 4 (over y, x), dp: 8 (over z, core).
Axes of the slice: x: 2, y: 2, z: 4, core: 2. Of those that a mesh axis runs over, the one named last changes fastest.
Arguments:
- observations: bfloat16 [64, 64, 4096], P('dp', None, 'group'), may hold values from -6 to 6
- next_observations: bfloat16 [1024, 4096], P('dp', 'group'), may hold values from -6 to 6
- trunk_weights: bfloat16 [2, 4096, 4096], P(None, 'dp', 'group'), may hold values from -0.125 to 0.125
- head_weights: bfloat16 [4096, 19], P('group'), may hold values from -0.25 to 0.25
- acting_policy_logits: float32 [64, 63, 18], P('dp'), may hold values from -16 to 330, as said below
- actions: int32 [64, 63], P('dp'), may hold values from 0 to 17
- rewards: float32 [64, 63], P('dp'), may hold values from -6 to 6
- episode_finished: int32 [64, 63], P('dp'), may hold values 0 or 1
Outputs:
- trunk_grads: float32 [2, 4096, 4096], P(None, 'dp', 'group')
- head_grads: float32 [4096, 19], P(('group', 'dp'))
- actor_logits: float32 [1024, 18], P('dp')
Inputs may be any that keep to these rules, and one draw needn't show every extreme that they name: `acting_policy_logits`: Real-valued scores, one row for each step and trajectory.
All inputs are finite; a program needn't handle non-finite values. No bound on the sum of `episode_finished` on one device may be relied on, other than what follows from the above.
Results may differ from a plain program's by a relative error of at most 0.012.
Values may be sent and summed in bfloat16 or wider, within the bound.
A program may use at most 128 MiB of HBM per device.

v0:
```python
import jax
import jax.numpy as jnp
from jax import lax
from jax.sharding import PartitionSpec as P

discount_rate = 0.99
value_weight = 0.5
entropy_weight = 0.1
loss_divisor = 16.0


def contract_rows(left, right):
    return lax.dot_general(
        left, right, (((0,), (0,)), ((), ())), preferred_element_type=jnp.float32
    )


def contract_cols(left, right):
    return lax.dot_general(
        left, right, (((1,), (1,)), ((), ())), preferred_element_type=jnp.float32
    )


def silu_slope(pre_value):
    sigma = jax.nn.sigmoid(pre_value)
    return sigma * (1.0 + pre_value * (1.0 - sigma))


def importance_trace_gradients(
    learner_output, acting_policy_logits, actions, rewards, episode_finished
):
    number_of_actions = acting_policy_logits.shape[-1]
    logits = learner_output[:, :, :number_of_actions]
    values = learner_output[:, :, number_of_actions]
    log_policy = jax.nn.log_softmax(logits[:, :-1], axis=-1)
    log_behave = jax.nn.log_softmax(acting_policy_logits, axis=-1)
    chosen = (
        actions[:, :, None] == jnp.arange(number_of_actions, dtype=jnp.int32)[None, None, :]
    ).astype(jnp.float32)
    ratio = jnp.exp(jnp.sum((log_policy - log_behave) * chosen, axis=-1))
    clipped = jnp.minimum(ratio, 1.0)
    discount = discount_rate * (1.0 - episode_finished.astype(jnp.float32))
    current = values[:, :-1]
    following = values[:, 1:]
    deltas = clipped * (rewards + discount * following - current)

    def backward_step(carried, step_item):
        delta_now, factor_now = step_item
        carried = delta_now + factor_now * carried
        return (carried, carried)

    start_carry = jnp.zeros((values.shape[0],), jnp.float32)
    _, corrections = lax.scan(
        backward_step, start_carry, (deltas.T, (discount * clipped).T), reverse=True
    )
    targets = current + corrections.T
    next_targets = jnp.concatenate([targets[:, 1:], values[:, -1:]], axis=1)
    advantage = clipped * (rewards + discount * next_targets - current)
    probability = jnp.exp(log_policy)
    entropy = -jnp.sum(probability * log_policy, axis=-1)
    logit_grad = (
        -advantage[..., None] * (chosen - probability)
        + entropy_weight * probability * (log_policy + entropy[..., None])
    ) / loss_divisor
    value_grad = -value_weight * (targets - current) / loss_divisor
    step_grad = jnp.concatenate([logit_grad, value_grad[..., None]], axis=-1)
    last_row = jnp.zeros((values.shape[0], 1, number_of_actions + 1), jnp.float32)
    return jnp.concatenate([step_grad, last_row], axis=1)


def per_device(
    observations,
    next_observations,
    trunk_weights,
    head_weights,
    acting_policy_logits,
    actions,
    rewards,
    episode_finished,
):
    traj_count, step_count, feature_block = observations.shape
    learner_rows = traj_count * step_count
    number_of_actions = acting_policy_logits.shape[-1]
    layer_total = trunk_weights.shape[0]
    own_rows = observations.reshape(learner_rows, feature_block)
    gathered_weights = [
        lax.all_gather(trunk_weights[layer_index], "dp", axis=0, tiled=True)
        for layer_index in range(layer_total)
    ]
    joined = jnp.concatenate([own_rows, next_observations], axis=0)
    inputs_full = []
    products_block = []
    current = joined
    for forward_layer_index in range(layer_total):
        forward_whole = lax.all_gather(current, "group", axis=1, tiled=True)
        inputs_full.append(forward_whole)
        product = jnp.dot(
            forward_whole, gathered_weights[forward_layer_index], preferred_element_type=jnp.float32
        )
        products_block.append(product)
        current = jax.nn.silu(product).astype(jnp.bfloat16)
    partial_head = jnp.dot(current, head_weights, preferred_element_type=jnp.float32)
    totals = lax.psum(partial_head, "group")
    inputs_full, products_block, last_block, totals = (inputs_full, products_block, current, totals)
    inputs_full = [whole[:learner_rows] for whole in inputs_full]
    products_block = [block[:learner_rows] for block in products_block]
    last_block = last_block[:learner_rows]
    head_out = totals[:learner_rows]
    actor_logits = totals[learner_rows:, :number_of_actions]
    learner_output = head_out.reshape(traj_count, step_count, number_of_actions + 1)
    output_gradient = importance_trace_gradients(
        learner_output, acting_policy_logits, actions, rewards, episode_finished
    )
    output_gradient = output_gradient.reshape(learner_rows, number_of_actions + 1).astype(
        jnp.bfloat16
    )
    head_partial = contract_rows(last_block, output_gradient)
    head_grads = lax.psum_scatter(head_partial, "dp", scatter_dimension=0, tiled=True)
    input_grad = contract_cols(output_gradient, head_weights)
    grad_list = [None] * layer_total
    for layer_index in range(layer_total - 1, -1, -1):
        pre_grad = (input_grad * silu_slope(products_block[layer_index])).astype(jnp.bfloat16)
        all_inputs = lax.all_to_all(
            inputs_full[layer_index], "dp", split_axis=1, concat_axis=0, tiled=True
        )
        all_upstream = lax.all_gather(pre_grad, "dp", axis=0, tiled=True)
        grad_list[layer_index] = contract_rows(all_inputs, all_upstream)
        if layer_index > 0:
            full_grad = contract_cols(pre_grad, gathered_weights[layer_index])
            input_grad = lax.psum_scatter(full_grad, "group", scatter_dimension=1, tiled=True)
    return (jnp.stack(grad_list), head_grads, actor_logits)


def solution(mesh):
    in_specs = (
        P("dp", None, "group"),
        P("dp", "group"),
        P(None, "dp", "group"),
        P("group", None),
        P("dp", None, None),
        P("dp", None),
        P("dp", None),
        P("dp", None),
    )
    out_specs = (P(None, "dp", "group"), P(("group", "dp"), None), P("dp", None))
    return jax.shard_map(
        per_device, mesh=mesh, in_specs=in_specs, out_specs=out_specs, check_vma=False
    )
```

profile of v0, /device:TPU:0, one launch (start us, length us, event | category | flops | bytes accessed | tf_op | source)
XLA Modules:
  0.0 727.3 jit_solution(5411754395285372085)
XLA Ops:
  7.2 2.6 pad_maximum_fusion.1
  12.3 62.2 %all-gather.9.cloned.1.call-done = bf16[640,4096]{1,0:T(8,128)(2,1)} async-done(((bf16[640,1024]{1,0:T(8,128)(2,1)}), bf16[640,4096]{1,0:T(8,128)(2,1)}) %all-gather.9.cloned.1.call-update) | async-done | bytes 5242896 | tf_op jit(solution)/shard_map/all_gather | solution.py:95
  74.5 83.7 %all-gather.17.cloned.1.call-done = bf16[1,4096,1024]{2,1,0:T(8,128)(2,1)} async-done(((bf16[1,512,1024]{2,1,0:T(8,128)(2,1)}), bf16[1,4096,1024]{2,1,0:T(8,128)(2,1)}) %all-gather.17.cloned.1.call-update) | async-done | bytes 8388624 | tf_op jit(solution)/shard_map/all_gather | solution.py:87
  158.1 10.7 %multiply_convert_fusion.1 = (bf16[640,1024]{1,0:T(8,128)(2,1)}, f32[640,1024]{1,0:T(8,128)S(1)}) fusion(bf16[640,4096]{1,0:T(8,128)(2,1)} %all-gather.9.cloned.1.call-done, bf16[1,4096,1024]{2,1,0:T(8,128)(2,1)} %all-gather.17.cloned.1.call-done), kind=kOutput, calls=%fused_computation.12 | convolution fusion | flops 5371985920 | bytes 17563648 | tf_op jit(solution)/shard_map/dot_general | solution.py:97
  169.1 71.2 %all-gather.19.cloned.1.call-done = bf16[1,4096,1024]{2,1,0:T(8,128)(2,1)} async-done(((bf16[1,512,1024]{2,1,0:T(8,128)(2,1)}), bf16[1,4096,1024]{2,1,0:T(8,128)(2,1)}) %all-gather.19.cloned.1.call-update) | async-done | bytes 8388624 | tf_op jit(solution)/shard_map/all_gather | solution.py:87
  240.3 62.1 %all-gather.11.cloned.1.call-done = bf16[640,4096]{1,0:T(8,128)(2,1)} async-done(((bf16[640,1024]{1,0:T(8,128)(2,1)}), bf16[640,4096]{1,0:T(8,128)(2,1)}) %all-gather.11.cloned.1.call-update) | async-done | bytes 5242896 | tf_op jit(solution)/shard_map/all_gather | solution.py:95
  302.4 10.9 %multiply_convert_fusion = (bf16[640,1024]{1,0:T(8,128)(2,1)S(1)}, f32[640,1024]{1,0:T(8,128)}) fusion(bf16[640,4096]{1,0:T(8,128)(2,1)} %all-gather.11.cloned.1.call-done, bf16[1,4096,1024]{2,1,0:T(8,128)(2,1)} %all-gather.19.cloned.1.call-done), kind=kOutput, calls=%fused_computation.11 | convolution fusion | flops 5371985920 | bytes 17563648 | tf_op jit(solution)/shard_map/dot_general | solution.py:97
  314.8 16.2 %psum.7 = f32[640,19]{0,1:T(8,128)S(1)} all-reduce(f32[640,19]{0,1:T(8,128)S(1)} %fusion.28), channel_id=1, replica_groups=mesh['group'=4,'dp'=8] {'group'}, use_global_device_ids=true, to_apply=%region_0.1 | all-reduce | flops 12160 | bytes 97280 | tf_op jit(solution)/shard_map/psum | solution.py:103
  331.5 4.7 while.17
  336.7 3.4 multiply_convert_fusion.3
  340.1 11.5 %fusion.2 = f32[512,4096]{1,0:T(8,128)} fusion(bf16[512,1024]{1,0:T(8,128)(2,1)} %multiply_convert_fusion.3, bf16[1,4096,1024]{2,1,0:T(8,128)(2,1)} %all-gather.19.cloned.1.call-done), kind=kOutput, calls=%fused_computation.3 | convolution fusion | flops 4294967296 | bytes 17825792 | tf_op jit(solution)/shard_map/dot_general | solution.py:19
  352.3 4.7 slice.62
  357.0 6.6 copy.47
  363.6 4.6 all-to-all-start
  368.4 69.6 %reduce-scatter.3.cloned.1.call-done = f32[512,1024]{1,0:T(8,128)} async-done(((f32[512,4096]{1,0:T(8,128)}), f32[512,1024]{1,0:T(8,128)}) %reduce-scatter.3.cloned.1.call-update) | async-done | bytes 2097168 | tf_op jit(solution)/shard_map/reduce_scatter | solution.py:130
  438.0 3.3 multiply_convert_fusion.2
  445.9 50.0 %all-to-all-done = bf16[512,8,512]{0,2,1:T(8,128)(2,1)} async-done(((bf16[512,8,512]{0,2,1:T(8,128)(2,1)}), bf16[512,8,512]{0,2,1:T(8,128)(2,1)}, u32[]{:S(2)}, u32[]{:S(2)}) %all-to-all-start) | async-done | bytes 4194336 | tf_op jit(solution)/shard_map/all_to_all | solution.py:123
  495.9 4.6 all-to-all-start.1
  500.5 6.6 copy.48
  508.7 146.3 %all-to-all-done.1 = bf16[512,8,512]{2,0,1:T(8,128)(2,1)} async-done(((bf16[512,8,512]{2,0,1:T(8,128)(2,1)}), bf16[512,8,512]{2,0,1:T(8,128)(2,1)}, u32[]{:S(2)}, u32[]{:S(2)}) %all-to-all-start.1) | async-done | bytes 4194336 | tf_op jit(solution)/shard_map/all_to_all | solution.py:123
  655.0 8.3 %convolution_bitcast_fusion = f32[1,512,1024]{2,1,0:T(8,128)S(1)} fusion(bf16[4096,512]{1,0:T(8,128)(2,1)} %bitcast.13, bf16[4096,1024]{1,0:T(8,128)(2,1)} %all-gather.15.cloned.1.call-done), kind=kOutput, calls=%fused_computation.15 | convolution fusion | flops 4294967296 | bytes 14680064 | tf_op jit(solution)/shard_map/dot_general | solution.py:13
  663.3 26.0 %all-gather.13.cloned.1.call-done = bf16[4096,1024]{1,0:T(8,128)(2,1)} async-done(((bf16[512,1024]{1,0:T(8,128)(2,1)}), bf16[4096,1024]{1,0:T(8,128)(2,1)}) %all-gather.13.cloned.1.call-update) | async-done | bytes 8388624 | tf_op jit(solution)/shard_map/all_gather | solution.py:126
  689.3 8.2 %convolution_bitcast_fusion.1 = f32[1,512,1024]{2,1,0:T(8,128)S(1)} fusion(bf16[4096,512]{1,0:T(8,128)(2,1)} %bitcast.68, bf16[4096,1024]{1,0:T(8,128)(2,1)} %all-gather.13.cloned.1.call-done), kind=kOutput, calls=%fused_computation.16 | convolution fusion | flops 4294967296 | bytes 14680064 | tf_op jit(solution)/shard_map/dot_general | solution.py:13
  700.0 20.5 %reduce-scatter.5.cloned.1.call-done = f32[128,19]{0,1:T(8,128)} async-done(((f32[1024,19]{0,1:T(8,128)}), f32[128,19]{0,1:T(8,128)}) %reduce-scatter.5.cloned.1.call-update) | async-done | bytes 9744 | tf_op jit(solution)/shard_map/reduce_scatter | solution.py:118
  (193 shorter events, 18.1 us)
Async XLA Ops:
  7.2 307.2 %copy-start = (bf16[1024,19]{0,1:T(8,128)(2,1)S(1)}, bf16[1024,19]{0,1:T(8,128)(2,1)}, u32[]{:S(2)}) copy-start(bf16[1024,19]{0,1:T(8,128)(2,1)} %param.14) | copy-start | bytes 116740
  7.2 2.7 copy-start.2
  7.2 67.3 %all-gather.9.cloned.1.call-start = ((), (), s32[]{:S(2)}) async-start(), calls=%async_computation.4 | async-start | bytes 6553600 | tf_op jit(solution)/shard_map/all_gather | solution.py:95
  9.9 148.3 %all-gather.17.cloned.1.call-start = ((), (), s32[]{:S(2)}) async-start(), calls=%async_computation.10 | async-start | bytes 9437184 | tf_op jit(solution)/shard_map/all_gather | solution.py:87
  11.5 228.8 %all-gather.19.cloned.1.call-start = ((), (), s32[]{:S(2)}) async-start(), calls=%async_computation.11 | async-start | bytes 9437184 | tf_op jit(solution)/shard_map/all_gather | solution.py:87
  12.2 156.8 %copy-start.5 = (f32[8,63,18]{1,0,2:T(8,128)S(1)}, f32[8,63,18]{1,0,2:T(8,128)}, u32[]{:S(2)}) copy-start(f32[8,63,18]{1,0,2:T(8,128)} %param.15) | copy-start | bytes 108868
  12.2 290.2 %all-gather.11.cloned.1.call-start = ((), (), s32[]{:S(2)}) async-start(), calls=%async_computation.5 | async-start | bytes 6553600 | tf_op jit(solution)/shard_map/all_gather | solution.py:95
  168.9 269.1 %reduce-scatter.3.cloned.1.call-start = ((), (), s32[]{:S(2)}) async-start(), calls=%async_computation.6 | async-start | bytes 10485760 | tf_op jit(solution)/shard_map/reduce_scatter | solution.py:130
  169.0 162.1 %copy-start.8 = (s32[8,63]{1,0:T(8,128)S(1)}, s32[8,63]{1,0:T(8,128)}, u32[]{:S(2)}) copy-start(s32[8,63]{1,0:T(8,128)} %param.16) | copy-start | bytes 6052
  169.0 162.2 %copy-start.6 = (s32[8,63]{1,0:T(8,128)S(1)}, s32[8,63]{1,0:T(8,128)}, u32[]{:S(2)}) copy-start(s32[8,63]{1,0:T(8,128)} %param.18) | copy-start | bytes 6052
  169.0 162.2 %copy-start.7 = (f32[8,63]{1,0:T(8,128)S(1)}, f32[8,63]{1,0:T(8,128)}, u32[]{:S(2)}) copy-start(f32[8,63]{1,0:T(8,128)} %param.17) | copy-start | bytes 6052
  313.3 1.1 copy-start.3
  351.7 303.3 %all-gather.15.cloned.1.call-start = ((), (), s32[]{:S(2)}) async-start(), calls=%async_computation.8 | async-start | bytes 9437184 | tf_op jit(solution)/shard_map/all_gather | solution.py:126
  363.6 132.3 %all-to-all-start = ((bf16[512,8,512]{0,2,1:T(8,128)(2,1)}), bf16[512,8,512]{0,2,1:T(8,128)(2,1)}, u32[]{:S(2)}, u32[]{:S(2)}) async-start(bf16[512,8,512]{0,2,1:T(8,128)(2,1)} %bitcast.65), calls=%async_computation | async-start | bytes 8388608 | tf_op jit(solution)/shard_map/all_to_all | solution.py:123
  368.2 321.1 %all-gather.13.cloned.1.call-start = ((), (), s32[]{:S(2)}) async-start(), calls=%async_computation.7 | async-start | bytes 9437184 | tf_op jit(solution)/shard_map/all_gather | solution.py:126
  441.3 2.2 slice-start
  495.9 159.1 %all-to-all-start.1 = ((bf16[512,8,512]{2,0,1:T(8,128)(2,1)}), bf16[512,8,512]{2,0,1:T(8,128)(2,1)}, u32[]{:S(2)}, u32[]{:S(2)}) async-start(bf16[512,8,512]{2,0,1:T(8,128)(2,1)} %bitcast.66), calls=%async_computation.2 | async-start | bytes 8388608 | tf_op jit(solution)/shard_map/all_to_all | solution.py:123
  500.5 220.0 %reduce-scatter.5.cloned.1.call-start = ((), (), s32[]{:S(2)}) async-start(), calls=%async_computation.9 | async-start | bytes 110592 | tf_op jit(solution)/shard_map/reduce_scatter | solution.py:118
  500.5 7.3 copy-start.4
  689.3 31.2 %copy-start.1 = (bf16[1024,19]{0,1:T(8,128)(2,1)S(1)}, bf16[1024,19]{0,1:T(8,128)(2,1)}, u32[]{:S(2)}) copy-start(bf16[1024,19]{0,1:T(8,128)(2,1)} %param.14) | copy-start | bytes 116740
Sparse Core Ops, SparseCore 0:
  10.4 64.0 all-gather.8
  76.1 82.0 all-gather.16
  159.7 80.5 all-gather.18
  242.6 59.7 all-gather.10
  351.8 86.1 reduce-scatter.2
  439.4 153.6 all-gather.14
  594.7 94.5 all-gather.12
  692.1 28.3 reduce-scatter.4
where the time goes:
time: 728 us; the launch traced here: 727 us
  waiting for transfers between devices  593 us (81%)
  matrix products  54.4 us (7%)
  local copies, waits for them, and re-layouts  28.9 us (4%)
  blocking collectives  16.2 us (2%)
  between operations  14.3 us (2%)
  other arithmetic  9.97 us (1%)
  starting transfers between devices  9.68 us (1%)
    all_to_all x2, waiting for transfers between devices, per_device(): lax.all_to_all(inputs_full[layer_index], 'dp', split_axis=1, concat_axis=...  196 us
    all_gather x2, waiting for transfers between devices, per_device(): lax.all_gather(trunk_weights[layer_index], 'dp', axis=0, tiled=True)  155 us
    all_gather x2, waiting for transfers between devices, per_device(): forward_whole = lax.all_gather(current, 'group', axis=1, tiled=True)  124 us
    reduce_scatter x1, waiting for transfers between devices, per_device(): lax.psum_scatter(full_grad, 'group', scatter_dimension=1, tiled=True)  69.6 us
    all_gather x2, waiting for transfers between devices, per_device(): all_upstream = lax.all_gather(pre_grad, 'dp', axis=0, tiled=True)  26 us
    dot_general x2, matrix products, per_device(): jnp.dot(forward_whole, gathered_weights[forward_layer_index], preferred_e...  21.6 us
    reduce_scatter x1, waiting for transfers between devices, per_device(): lax.psum_scatter(head_partial, 'dp', scatter_dimension=0, tiled=True)  20.5 us
    dot_general x3, matrix products, contract_rows(): lax.dot_general(left, right, (((0,), (0,)), ((), ())), preferred_element_...  17.4 us
  transfers between devices with their start and end apart: 10, of which 9 were waited for; matrix products, arithmetic and copies ran while one was open for 8% of the time, Pallas kernels for 0%

commit v1 on v0

--- a/solution.py
+++ b/solution.py
@@ -120,8 +120,14 @@
     grad_list = [None] * layer_total
     for layer_index in range(layer_total - 1, -1, -1):
         pre_grad = (input_grad * silu_slope(products_block[layer_index])).astype(jnp.bfloat16)
-        all_inputs = lax.all_to_all(
-            inputs_full[layer_index], "dp", split_axis=1, concat_axis=0, tiled=True
+        all_inputs = jnp.concatenate(
+            lax.all_to_all(
+                jnp.stack(jnp.split(inputs_full[layer_index], lax.axis_size("dp"), axis=1)),
+                "dp",
+                0,
+                0,
+            ),
+            axis=0,
         )
         all_upstream = lax.all_gather(pre_grad, "dp", axis=0, tiled=True)
         grad_list[layer_index] = contract_rows(all_inputs, all_upstream)

time: 728 us -> 793 us (1.089)
  waiting for transfers between devices: 593 us -> 650 us
    all_to_all x2, waiting for transfers between devices: 196 us -> 282 us  [per_device(): lax.all_to_all(jnp.stack(jnp.split(inputs_full[layer_index], lax.axis_siz...]
    unnamed x20 -> x34, local copies, waits for them, and re-layouts: 1.31 us -> 27.7 us
    all_gather x2, waiting for transfers between devices: 26 us -> 0.02 us  [per_device(): all_upstream = lax.all_gather(pre_grad, 'dp', axis=0, tiled=True)]
    slice x4 -> x0, local copies, waits for them, and re-layouts: 13.5 us -> none  [per_device(): inputs_full = [whole[:learner_rows] for whole in inputs_full]]
    reduce_scatter x1, waiting for transfers between devices: 20.5 us -> 7.62 us  [per_device(): lax.psum_scatter(head_partial, 'dp', scatter_dimension=0, tiled=True)]
    reduce_scatter x1, waiting for transfers between devices: 69.6 us -> 80 us  [per_device(): lax.psum_scatter(full_grad, 'group', scatter_dimension=1, tiled=True)]
    all_to_all x2 -> x0, local copies, waits for them, and re-layouts: 9.06 us -> none  [per_device(): lax.all_to_all(inputs_full[layer_index], 'dp', split_axis=1, concat_axis=...]
  transfers between devices with their start and end apart: 10 -> 10, of which waited for: 9 -> 8; matrix products, arithmetic and copies ran while one was open for 8% -> 8% of each run, Pallas kernels for 0% -> 0%
where the time goes in v1:
time: 793 us; the launch traced here: 792 us
  waiting for transfers between devices  650 us (82%)
  matrix products  54.4 us (7%)
  local copies, waits for them, and re-layouts  36.5 us (5%)
  blocking collectives  16.2 us (2%)
  between operations  14.3 us (2%)
  other arithmetic  9.99 us (1%)
  starting transfers between devices  9.61 us (1%)
    all_to_all x2, waiting for transfers between devices, per_device(): lax.all_to_all(jnp.stack(jnp.split(inputs_full[layer_index], lax.axis_siz...  282 us
    all_gather x2, waiting for transfers between devices, per_device(): lax.all_gather(trunk_weights[layer_index], 'dp', axis=0, tiled=True)  155 us
    all_gather x2, waiting for transfers between devices, per_device(): forward_whole = lax.all_gather(current, 'group', axis=1, tiled=True)  124 us
    reduce_scatter x1, waiting for transfers between devices, per_device(): lax.psum_scatter(full_grad, 'group', scatter_dimension=1, tiled=True)  80 us
    unnamed x34, local copies, waits for them, and re-layouts  27.7 us
    dot_general x2, matrix products, per_device(): jnp.dot(forward_whole, gathered_weights[forward_layer_index], preferred_e...  21.6 us
    dot_general x3, matrix products, contract_rows(): lax.dot_general(left, right, (((0,), (0,)), ((), ())), preferred_element_...  17.4 us
    psum x1, blocking collectives, per_device(): totals = lax.psum(partial_head, 'group')  16.2 us
  transfers between devices with their start and end apart: 10, of which 8 were waited for; matrix products, arithmetic and copies ran while one was open for 8% of the time, Pallas kernels for 0%

profile of v1, /device:TPU:0, one launch (start us, length us, event | category | flops | bytes accessed | tf_op | source)
XLA Modules:
  0.0 792.2 jit_solution(13268909748593313328)
XLA Ops:
  7.2 2.6 pad_maximum_fusion.1
  12.3 62.2 %all-gather.9.cloned.1.call-done = bf16[640,4096]{1,0:T(8,128)(2,1)} async-done(((bf16[640,1024]{1,0:T(8,128)(2,1)}), bf16[640,4096]{1,0:T(8,128)(2,1)}) %all-gather.9.cloned.1.call-update) | async-done | bytes 5242896 | tf_op jit(solution)/shard_map/all_gather | solution.py:95
  74.5 83.7 %all-gather.17.cloned.1.call-done = bf16[1,4096,1024]{2,1,0:T(8,128)(2,1)} async-done(((bf16[1,512,1024]{2,1,0:T(8,128)(2,1)}), bf16[1,4096,1024]{2,1,0:T(8,128)(2,1)}) %all-gather.17.cloned.1.call-update) | async-done | bytes 8388624 | tf_op jit(solution)/shard_map/all_gather | solution.py:87
  158.1 10.7 %multiply_convert_fusion.1 = (bf16[640,1024]{1,0:T(8,128)(2,1)}, f32[640,1024]{1,0:T(8,128)S(1)}) fusion(bf16[640,4096]{1,0:T(8,128)(2,1)} %all-gather.9.cloned.1.call-done, bf16[1,4096,1024]{2,1,0:T(8,128)(2,1)} %all-gather.17.cloned.1.call-done), kind=kOutput, calls=%fused_computation.11 | convolution fusion | flops 5371985920 | bytes 17563648 | tf_op jit(solution)/shard_map/dot_general | solution.py:97
  169.1 71.2 %all-gather.19.cloned.1.call-done = bf16[1,4096,1024]{2,1,0:T(8,128)(2,1)} async-done(((bf16[1,512,1024]{2,1,0:T(8,128)(2,1)}), bf16[1,4096,1024]{2,1,0:T(8,128)(2,1)}) %all-gather.19.cloned.1.call-update) | async-done | bytes 8388624 | tf_op jit(solution)/shard_map/all_gather | solution.py:87
  240.3 62.1 %all-gather.11.cloned.1.call-done = bf16[640,4096]{1,0:T(8,128)(2,1)} async-done(((bf16[640,1024]{1,0:T(8,128)(2,1)}), bf16[640,4096]{1,0:T(8,128)(2,1)}) %all-gather.11.cloned.1.call-update) | async-done | bytes 5242896 | tf_op jit(solution)/shard_map/all_gather | solution.py:95
  302.4 10.9 %multiply_convert_fusion = (bf16[640,1024]{1,0:T(8,128)(2,1)S(1)}, f32[640,1024]{1,0:T(8,128)}) fusion(bf16[640,4096]{1,0:T(8,128)(2,1)} %all-gather.11.cloned.1.call-done, bf16[1,4096,1024]{2,1,0:T(8,128)(2,1)} %all-gather.19.cloned.1.call-done), kind=kOutput, calls=%fused_computation.10 | convolution fusion | flops 5371985920 | bytes 17563648 | tf_op jit(solution)/shard_map/dot_general | solution.py:97
  314.8 16.2 %psum.7 = f32[640,19]{0,1:T(8,128)S(1)} all-reduce(f32[640,19]{0,1:T(8,128)S(1)} %fusion.44), channel_id=1, replica_groups=mesh['group'=4,'dp'=8] {'group'}, use_global_device_ids=true, to_apply=%region_0.1 | all-reduce | flops 12160 | bytes 97280 | tf_op jit(solution)/shard_map/psum | solution.py:103
  331.5 4.7 while.17
  336.7 3.4 multiply_convert_fusion.3
  340.1 11.5 %fusion.2 = f32[512,4096]{1,0:T(8,128)} fusion(bf16[512,1024]{1,0:T(8,128)(2,1)} %multiply_convert_fusion.3, bf16[1,4096,1024]{2,1,0:T(8,128)(2,1)} %all-gather.19.cloned.1.call-done), kind=kOutput, calls=%fused_computation.3 | convolution fusion | flops 4294967296 | bytes 17825792 | tf_op jit(solution)/shard_map/dot_general | solution.py:19
  357.9 80.0 %reduce-scatter.3.cloned.1.call-done = f32[512,1024]{1,0:T(8,128)} async-done(((f32[512,4096]{1,0:T(8,128)}), f32[512,1024]{1,0:T(8,128)}) %reduce-scatter.3.cloned.1.call-update) | async-done | bytes 2097168 | tf_op jit(solution)/shard_map/reduce_scatter | solution.py:136
  437.9 3.4 multiply_convert_fusion.2
  445.0 1.9 fusion.12
  446.9 1.9 fusion.11
  448.9 1.9 fusion.10
  450.8 4.7 all-to-all-start.1
  470.6 138.9 %all-to-all-done.1 = bf16[8,512,512]{2,1,0:T(8,128)(2,1)} async-done(((bf16[8,512,512]{2,1,0:T(8,128)(2,1)}), bf16[8,512,512]{2,1,0:T(8,128)(2,1)}, u32[]{:S(2)}, u32[]{:S(2)}) %all-to-all-start.1) | async-done | bytes 4194336 | tf_op jit(solution)/shard_map/all_to_all | solution.py:124
  609.5 4.5 all-to-all-start
  615.6 8.3 %convolution_bitcast_fusion = f32[1,512,1024]{2,1,0:T(8,128)S(1)} fusion(bf16[4096,512]{1,0:T(8,128)(2,1)} %bitcast.26, bf16[4096,1024]{1,0:T(8,128)(2,1)} %all-gather.15.cloned.1.call-done), kind=kOutput, calls=%fused_computation.14 | convolution fusion | flops 4294967296 | bytes 14680064 | tf_op jit(solution)/shard_map/dot_general | solution.py:13
  623.9 143.1 %all-to-all-done = bf16[8,512,512]{2,1,0:T(8,128)(2,1)} async-done(((bf16[8,512,512]{2,1,0:T(8,128)(2,1)}), bf16[8,512,512]{2,1,0:T(8,128)(2,1)}, u32[]{:S(2)}, u32[]{:S(2)}) %all-to-all-start) | async-done | bytes 4194336 | tf_op jit(solution)/shard_map/all_to_all | solution.py:124
  767.0 8.2 %convolution_bitcast_fusion.1 = f32[1,512,1024]{2,1,0:T(8,128)S(1)} fusion(bf16[4096,512]{1,0:T(8,128)(2,1)} %bitcast.9, bf16[4096,1024]{1,0:T(8,128)(2,1)} %all-gather.13.cloned.1.call-done), kind=kOutput, calls=%fused_computation.15 | convolution fusion | flops 4294967296 | bytes 14680064 | tf_op jit(solution)/shard_map/dot_general | solution.py:13
  775.3 2.5 pad_maximum_fusion
  777.7 7.6 reduce-scatter.5.cloned.1.call-done
  (203 shorter events, 35.3 us)
Async XLA Ops:
  7.2 307.1 %copy-start = (bf16[1024,19]{0,1:T(8,128)(2,1)S(1)}, bf16[1024,19]{0,1:T(8,128)(2,1)}, u32[]{:S(2)}) copy-start(bf16[1024,19]{0,1:T(8,128)(2,1)} %param.14) | copy-start | bytes 116740
  7.2 2.7 copy-start.2
  7.2 67.3 %all-gather.9.cloned.1.call-start = ((), (), s32[]{:S(2)}) async-start(), calls=%async_computation.4 | async-start | bytes 6553600 | tf_op jit(solution)/shard_map/all_gather | solution.py:95
  9.9 148.3 %all-gather.17.cloned.1.call-start = ((), (), s32[]{:S(2)}) async-start(), calls=%async_computation.10 | async-start | bytes 9437184 | tf_op jit(solution)/shard_map/all_gather | solution.py:87
  11.5 228.8 %all-gather.19.cloned.1.call-start = ((), (), s32[]{:S(2)}) async-start(), calls=%async_computation.11 | async-start | bytes 9437184 | tf_op jit(solution)/shard_map/all_gather | solution.py:87
  12.2 156.8 %copy-start.5 = (f32[8,63,18]{1,0,2:T(8,128)S(1)}, f32[8,63,18]{1,0,2:T(8,128)}, u32[]{:S(2)}) copy-start(f32[8,63,18]{1,0,2:T(8,128)} %param.15) | copy-start | bytes 108868
  12.2 290.2 %all-gather.11.cloned.1.call-start = ((), (), s32[]{:S(2)}) async-start(), calls=%async_computation.5 | async-start | bytes 6553600 | tf_op jit(solution)/shard_map/all_gather | solution.py:95
  168.9 269.0 %reduce-scatter.3.cloned.1.call-start = ((), (), s32[]{:S(2)}) async-start(), calls=%async_computation.6 | async-start | bytes 10485760 | tf_op jit(solution)/shard_map/reduce_scatter | solution.py:136
  169.0 162.2 %copy-start.8 = (s32[8,63]{1,0:T(8,128)S(1)}, s32[8,63]{1,0:T(8,128)}, u32[]{:S(2)}) copy-start(s32[8,63]{1,0:T(8,128)} %param.16) | copy-start | bytes 6052
  169.0 162.2 %copy-start.6 = (s32[8,63]{1,0:T(8,128)S(1)}, s32[8,63]{1,0:T(8,128)}, u32[]{:S(2)}) copy-start(s32[8,63]{1,0:T(8,128)} %param.18) | copy-start | bytes 6052
  169.0 162.2 %copy-start.7 = (f32[8,63]{1,0:T(8,128)S(1)}, f32[8,63]{1,0:T(8,128)}, u32[]{:S(2)}) copy-start(f32[8,63]{1,0:T(8,128)} %param.17) | copy-start | bytes 6052
  313.3 1.1 copy-start.3
  351.6 264.0 %all-gather.15.cloned.1.call-start = ((), (), s32[]{:S(2)}) async-start(), calls=%async_computation.8 | async-start | bytes 9437184 | tf_op jit(solution)/shard_map/all_gather | solution.py:132
  352.2 414.8 %all-gather.13.cloned.1.call-start = ((), (), s32[]{:S(2)}) async-start(), calls=%async_computation.7 | async-start | bytes 9437184 | tf_op jit(solution)/shard_map/all_gather | solution.py:132
  450.8 158.7 %all-to-all-start.1 = ((bf16[8,512,512]{2,1,0:T(8,128)(2,1)}), bf16[8,512,512]{2,1,0:T(8,128)(2,1)}, u32[]{:S(2)}, u32[]{:S(2)}) async-start(bf16[8,512,512]{2,1,0:T(8,128)(2,1)} %fusion.10), calls=%async_computation.2 | async-start | bytes 8388608 | tf_op jit(solution)/shard_map/all_to_all | solution.py:124
  470.6 144.1 %copy-start.4 = (bf16[640,1024]{1,0:T(8,128)(2,1)S(1)}, bf16[640,1024]{1,0:T(8,128)(2,1)}, u32[]{:S(2)}) copy-start(bf16[640,1024]{1,0:T(8,128)(2,1)} %copy-done.3) | copy-start | bytes 3932164
  609.5 157.5 %all-to-all-start = ((bf16[8,512,512]{2,1,0:T(8,128)(2,1)}), bf16[8,512,512]{2,1,0:T(8,128)(2,1)}, u32[]{:S(2)}, u32[]{:S(2)}) async-start(bf16[8,512,512]{2,1,0:T(8,128)(2,1)} %fusion.18), calls=%async_computation | async-start | bytes 8388608 | tf_op jit(solution)/shard_map/all_to_all | solution.py:124
  614.0 171.3 %reduce-scatter.5.cloned.1.call-start = ((), (), s32[]{:S(2)}) async-start(), calls=%async_computation.9 | async-start | bytes 110592 | tf_op jit(solution)/shard_map/reduce_scatter | solution.py:118
  767.0 18.3 %copy-start.1 = (bf16[1024,19]{0,1:T(8,128)(2,1)S(1)}, bf16[1024,19]{0,1:T(8,128)(2,1)}, u32[]{:S(2)}) copy-start(bf16[1024,19]{0,1:T(8,128)(2,1)} %param.14) | copy-start | bytes 116740
Sparse Core Ops, SparseCore 0:
  10.4 64.0 all-gather.8
  76.1 82.0 all-gather.16
  159.7 80.5 all-gather.18
  242.6 59.7 all-gather.10
  351.8 86.0 reduce-scatter.2
  439.3 157.2 all-gather.14
  598.2 155.3 all-gather.12
  756.4 28.8 reduce-scatter.4
